TPU v7x, 32 devices: a whole 2x2x4 slice. The times are simulated.
32 devices in a mesh: groups: 2 (over y), seq: 4 (over z), exp: 2 (over x), tp: 2 (over core).
Axes of the slice: x: 2, y: 2, z: 4, core: 2. Of those that a mesh axis runs over, the one named last changes fastest.
Arguments:
- attn_query: bfloat16 [2048, 1152], P(('groups', 'seq'), ('exp', 'tp')), parts along dimension 0, may hold values from -6 to 6
- fresh_keys: bfloat16 [2048, 1152], P(('groups', 'seq'), ('exp', 'tp')), parts along dimension 0, may hold values from -6 to 6
- fresh_values: bfloat16 [2048, 1152], P(('groups', 'seq'), ('exp', 'tp')), parts along dimension 0, may hold values from -6 to 6
- stale_keys: bfloat16 [2048, 1152], P(('groups', 'seq'), ('exp', 'tp')), parts along dimension 0, may hold values from -6 to 6
- stale_values: bfloat16 [2048, 1152], P(('groups', 'seq'), ('exp', 'tp')), parts along dimension 0, may hold values from -6 to 6
- block_flags: int32 [16], P(('groups', 'seq')), parts along dimension 0, may hold values 0 or 1
- moe_tokens: bfloat16 [4096, 1152], P(('groups', 'seq', 'exp', 'tp')), parts along dimension 0, may hold values from -6 to 6
- expert_ids: int32 [4096, 2], P(('groups', 'seq', 'exp', 'tp')), parts along dimension 0, may hold values from 0 to 3, all different within a row; in each aligned block of 128 rows (0 to 127, 128 to 255, ...) at most 80 rows name the same one
- gate_weights: float32 [4096, 2], P(('groups', 'seq', 'exp', 'tp')), parts along dimension 0, may hold values from 0.25 to 1
- up_weight: bfloat16 [4, 1152, 4608], P('seq', None, ('exp', 'tp')), may hold values from -0.1875 to 0.1875
- up_bias: float32 [4, 4608], P('seq', ('exp', 'tp')), may hold values from -3 to 3
- down_weight: bfloat16 [4, 4608, 1152], P('seq', ('exp', 'tp')), may hold values from -0.09375 to 0.09375
- down_bias: float32 [4, 1152], P('seq'), may hold values from -2 to 2
Outputs:
- attn_out: bfloat16 [2048, 1152], P(('groups', 'seq'), ('exp', 'tp')), parts along dimension 0
- moe_out: bfloat16 [4096, 1152], P(('groups', 'seq', 'exp', 'tp')), parts along dimension 0
There are 2 independent parts, one for each index of `groups`. A program takes and returns all parts, laid end to end along the dimension named above; an argument that names none is the same for every part. Nothing has to cross between parts.
Inputs may be any that keep to these rules, and one draw needn't show every extreme that they name: `expert_ids`: the 2 ids of a token differ. In the rows of one device no expert is named more than 80 times, and in every draw some expert is named exactly 80 times in some device's rows.
All inputs are finite; a program needn't handle non-finite values. No bound on the sum of `block_flags` on one device may be relied on, other than what follows from the above.
Results may differ from a plain program's by a relative error of at most 0.014.
Values may be sent and summed in bfloat16 or wider, within the bound.
A program may use at most 64 MiB of HBM per device.

v0:
```python
import functools
import math

import jax
import jax.numpy as jnp
from jax import lax
from jax.experimental import pallas as pl
from jax.experimental.pallas import tpu as pltpu
from jax.sharding import PartitionSpec as P

HD = 72
MESH = pl.DeviceIdType.MESH
F32 = jnp.float32
BF16 = jnp.bfloat16


def layer_kernel(
    sizes,
    q_ref, fresh_k, fresh_v, stale_k, stale_v, flags,
    tok_ref, ids_ref, gate_ref,
    up_hbm, upb_ref, down_hbm, downb_ref,
    attn_ref, moe_ref,
    up_v, down_v, place_v, disp, rows, tpin, xin, fin, ret, kv, keys_v, acc, turn,
    w_sem,
    z_send, z_recv, xf_send, xf_recv, tf_send, tf_recv,
    tr_send, tr_recv, xr_send, xr_recv, zr_send, zr_recv, kv_right, kv_left, kv_recv,
):
    S, X, capp = sizes
    s, x, c = lax.axis_index("seq"), lax.axis_index("exp"), lax.axis_index("tp")
    oc = 1 - c
    T, D = tok_ref.shape
    W, L = q_ref.shape
    heads = W // HD
    blk = L // flags.shape[0]

    up_copy = pltpu.make_async_copy(up_hbm.at[0], up_v, w_sem.at[0])
    down_copy = pltpu.make_async_copy(down_hbm.at[0], down_v, w_sem.at[1])
    up_copy.start()
    down_copy.start()

    def rdma(src, dst, ssem, rsem, where):
        return pltpu.make_async_remote_copy(
            src_ref=src, dst_ref=dst, send_sem=ssem, recv_sem=rsem,
            device_id=where, device_id_type=MESH,
        )

    def z_copy(e, slot):
        return rdma(disp.at[e], rows.at[slot, c, x], z_send.at[e], z_recv.at[slot], {"seq": e})

    def x_forward(src, to, origin):
        return rdma(
            rows.at[src, c, origin], rows.at[src, c, origin],
            xf_send.at[src, to], xf_recv.at[src, origin], {"exp": to},
        )

    def t_forward(src, origin, side):
        return rdma(
            rows.at[src, side, origin], rows.at[src, side, origin],
            tf_send.at[src, origin], tf_recv.at[src, origin], {"tp": oc},
        )

    def t_reduce(src):
        return rdma(rows.at[src, oc], tpin.at[src], tr_send.at[src], tr_recv.at[src], {"tp": oc})

    def x_reduce(src, to, origin):
        return rdma(
            rows.at[src, c, to], xin.at[src, origin],
            xr_send.at[src, to], xr_recv.at[src, origin], {"exp": to},
        )

    def z_return(src, slot):
        return rdma(fin.at[src], ret.at[slot], zr_send.at[src], zr_recv.at[slot], {"seq": src})

    def kv_copy(b, step):
        sems = kv_right if step > 0 else kv_left
        return rdma(kv.at[b], kv.at[b], sems.at[b], kv_recv.at[b], {"seq": s + step})

    def other_x(i):
        return lax.rem(x + i, X)

    def order(k):
        side = jnp.minimum(s, S - 1 - s)
        near = k // 2 + 1
        near = jnp.where(lax.rem(k, 2) == 0, near, -near)
        far = k - side + 1
        far = jnp.where(2 * s < S, far, -far)
        step = jnp.where(k < 2 * side, near, far)
        return s + jnp.where(k == S - 1, 0, step)

    barrier = pltpu.get_barrier_semaphore()
    for i in range(1, S):
        pl.semaphore_signal(barrier, inc=1, device_id={"seq": lax.rem(s + i, S)}, device_id_type=MESH)
    for i in range(1, X):
        pl.semaphore_signal(barrier, inc=1, device_id={"exp": other_x(i)}, device_id_type=MESH)
    pl.semaphore_signal(barrier, inc=1, device_id={"tp": oc}, device_id_type=MESH)

    expert = lax.broadcasted_iota(jnp.int32, (S, T), 0)
    named = (ids_ref[0:1, :] == expert) | (ids_ref[1:2, :] == expert)
    earlier = lax.broadcasted_iota(jnp.int32, (T, T), 0) < lax.broadcasted_iota(jnp.int32, (T, T), 1)
    place = jnp.dot(
        jnp.where(named, 1.0, 0.0).astype(BF16),
        jnp.where(earlier, 1.0, 0.0).astype(BF16),
        preferred_element_type=F32,
    )
    place_v[...] = jnp.where(named, place, -1.0)
    slot_rows = lax.broadcasted_iota(jnp.int32, (capp, T), 0).astype(F32)

    def slots_of(e):
        pick = jnp.where(place_v[pl.ds(e, 1), :] == slot_rows, 1.0, 0.0).astype(BF16)
        return jnp.dot(pick, tok_ref[...], preferred_element_type=F32).astype(BF16)

    def forward(src):
        for i in range(1, X):
            x_forward(src, other_x(i), x).start()
        t_forward(src, x, c).start()

    rows[s, c, x] = slots_of(s)
    pl.semaphore_wait(barrier, S - 1 + X - 1 + 1)
    forward(s)
    def dispatch(k):
        e = order(jnp.int32(k))
        disp[e] = slots_of(e)
        z_copy(e, s).start()

    for k in range(min(2, S - 1)):
        dispatch(k)
    for b in range(flags.shape[0]):
        fresh = flags[b] == 1
        part = pl.ds(b * blk, blk)
        kv[s, 0, :, part] = jnp.where(fresh, fresh_k[:, part], stale_k[:, part])
        kv[s, 1, :, part] = jnp.where(fresh, fresh_v[:, part], stale_v[:, part])

    def relay(step):
        low, high = s - (step - 1), s + (step - 1)

        @pl.when(low >= 0)
        def _():
            @pl.when(low < s)
            def _():
                kv_copy(low, 1).wait_recv()

            @pl.when(s + 1 < S)
            def _():
                kv_copy(low, 1).start()

        @pl.when(high < S)
        def _():
            @pl.when(high > s)
            def _():
                kv_copy(high, -1).wait_recv()

            @pl.when(s - 1 >= 0)
            def _():
                kv_copy(high, -1).start()

    relay(1)
    for k in range(2, S - 1):
        dispatch(k)
    nearest = order(jnp.int32(0))
    z_copy(nearest, nearest).wait_recv()
    forward(nearest)

    up_copy.wait()
    down_copy.wait()

    def finish(src):
        total = rows[src, c, x].astype(F32) + downb_ref[...]
        for i in range(1, X):
            x_reduce(src, other_x(i), other_x(i)).wait_recv()
            total = total + xin[src, other_x(i)].astype(F32)
        done = total.astype(BF16)
        fin[src] = done

    def finish_send(src):
        finish(src)

        @pl.when(src != s)
        def _():
            z_return(src, s).start()

        @pl.when(src == s)
        def _():
            ret[s] = fin[s]

    def chunk(k, unused):
        src = order(k)
        for i in range(1, X):
            x_forward(src, other_x(i), other_x(i)).wait_recv()
            t_forward(src, other_x(i), c).start()

        @pl.when(k + 1 < S - 1)
        def _():
            nxt = order(k + 1)
            z_copy(nxt, nxt).wait_recv()
            forward(nxt)

        for i in range(X):
            t_forward(src, other_x(i), oc).wait_recv()
        for i in range(1, X):
            x_forward(src, other_x(i), x).wait_send()
        for i in range(X):
            t_forward(src, other_x(i), c).wait_send()

        block = rows[src].reshape(2 * X * capp, D)
        hidden = jnp.dot(block, up_v[...], preferred_element_type=F32) + upb_ref[...]
        hidden = jax.nn.gelu(hidden).astype(BF16)
        result = jnp.dot(hidden, down_v[...], preferred_element_type=F32).astype(BF16)
        rows[src] = result.reshape(2, X, capp, D)
        t_reduce(src).start()

        @pl.when(k >= 1)
        def _():
            finish_send(order(k - 1))

        @pl.when(k == 0)
        def _():
            relay(2)

        @pl.when((k >= 2) & (k < S - 1))
        def _():
            relay(k + 1)

        t_reduce(src).wait_recv()
        for i in range(X):
            to = other_x(i)
            rows[src, c, to] = (rows[src, c, to].astype(F32) + tpin[src, to].astype(F32)).astype(BF16)
            if i > 0:
                x_reduce(src, to, x).start()
        return unused

    lax.fori_loop(0, S, chunk, jnp.int32(0))

    relay(S)

    for i in range(S):
        keys_v[pl.ds(i * L, L), :] = kv[i, 0].T
    scale = 1.0 / math.sqrt(HD)
    channel = lax.broadcasted_iota(jnp.int32, (W, L), 0)

    def head(h, unused):
        mine = (channel >= h * HD) & (channel < (h + 1) * HD)
        query = jnp.where(mine, q_ref[...].astype(F32), 0.0).astype(BF16)
        scores = jnp.dot(keys_v[...], query, preferred_element_type=F32) * scale
        probs = jnp.exp(scores - jnp.max(scores, axis=0, keepdims=True))
        total = jnp.sum(probs, axis=0, keepdims=True)
        weights = probs.astype(BF16)
        mixed = jnp.zeros((W, L), F32)
        for i in range(S):
            mixed += jnp.dot(kv[i, 1], weights[i * L : (i + 1) * L], preferred_element_type=F32)
        acc[...] = jnp.where(mine, mixed / total, acc[...])
        return unused

    acc[...] = jnp.zeros_like(acc)
    lax.fori_loop(0, heads, head, jnp.int32(0))
    attn_ref[...] = acc[...].astype(BF16)
    finish_send(s)

    base = jnp.where(named, place, 0.0) + (expert * capp).astype(F32)
    turn[...] = jnp.zeros_like(turn)
    for j in range(2):
        hit = ids_ref[j : j + 1, :] == expert
        turn[j : j + 1, :] = jnp.sum(jnp.where(hit, base, 0.0), axis=0, keepdims=True)
        turn[2 + j : 3 + j, :] = gate_ref[j : j + 1, :]
    turned = turn[...].T
    slot_lane = lax.broadcasted_iota(jnp.int32, (T, S * capp), 1).astype(F32)
    picks = [jnp.where(turned[:, j : j + 1] == slot_lane, 1.0, 0.0).astype(BF16) for j in range(2)]
    for i in range(1, S):
        z_return(s, lax.rem(s + i, S)).wait_recv()
    everything = ret[...].reshape(S * capp, D)
    moe_ref[...] = (
        jnp.dot(picks[0], everything, preferred_element_type=F32) * turned[:, 2:3]
        + jnp.dot(picks[1], everything, preferred_element_type=F32) * turned[:, 3:4]
    ).astype(BF16)

    def drain(i, unused):
        to = lax.rem(s + i, S)
        z_copy(to, s).wait_send()
        z_return(to, s).wait_send()
        return unused

    lax.fori_loop(1, S, drain, jnp.int32(0))

    def drain_chunk(i, unused):
        t_reduce(i).wait_send()
        for j in range(1, X):
            x_reduce(i, other_x(j), x).wait_send()

        @pl.when((i <= s) & (s + 1 < S))
        def _():
            kv_copy(i, 1).wait_send()

        @pl.when((i >= s) & (s - 1 >= 0))
        def _():
            kv_copy(i, -1).wait_send()

        return unused

    lax.fori_loop(0, S, drain_chunk, jnp.int32(0))


def local(
    attn_query, fresh_keys, fresh_values, stale_keys, stale_values, block_flags,
    moe_tokens, expert_ids, gate_weights, up_weight, up_bias, down_weight, down_bias,
):
    S, X = lax.axis_size("seq"), lax.axis_size("exp")
    assert lax.axis_size("tp") == 2 and up_weight.shape[0] == 1
    tokens, D = moe_tokens.shape
    length, width = attn_query.shape
    hidden = up_weight.shape[2]
    cap = 5 * tokens // (2 * S)
    capp = -(-cap // 16) * 16
    vmem = pl.BlockSpec(memory_space=pltpu.VMEM)
    smem = pl.BlockSpec(memory_space=pltpu.SMEM)
    hbm = pl.BlockSpec(memory_space=pl.ANY)
    dma = pltpu.SemaphoreType.DMA
    attn_out, moe_out = pl.pallas_call(
        functools.partial(layer_kernel, (S, X, capp)),
        out_shape=(
            jax.ShapeDtypeStruct((width, length), BF16),
            jax.ShapeDtypeStruct((tokens, D), BF16),
        ),
        in_specs=[vmem] * 5 + [smem] + [vmem] * 3 + [hbm, vmem, hbm, vmem],
        out_specs=(vmem, vmem),
        scratch_shapes=[
            pltpu.VMEM((D, hidden), BF16),
            pltpu.VMEM((hidden, D), BF16),
            pltpu.VMEM((S, tokens), F32),
            pltpu.VMEM((S, capp, D), BF16),
            pltpu.VMEM((S, 2, X, capp, D), BF16),
            pltpu.VMEM((S, X, capp, D), BF16),
            pltpu.VMEM((S, X, capp, D), BF16),
            pltpu.VMEM((S, capp, D), BF16),
            pltpu.VMEM((S, capp, D), BF16),
            pltpu.VMEM((S, 2, width, length), BF16),
            pltpu.VMEM((S * length, width), BF16),
            pltpu.VMEM((width, length), F32),
            pltpu.VMEM((128, tokens), F32),
            dma((2,)),
            dma((S,)), dma((S,)), dma((S, X)), dma((S, X)), dma((S, X)), dma((S, X)),
            dma((S,)), dma((S,)), dma((S, X)), dma((S, X)), dma((S,)), dma((S,)),
            dma((S,)), dma((S,)), dma((S,)),
        ],
        compiler_params=pltpu.CompilerParams(
            collective_id=0, has_side_effects=True, vmem_limit_bytes=67043328
        ),
    )(
        attn_query.T, fresh_keys.T, fresh_values.T, stale_keys.T, stale_values.T, block_flags,
        moe_tokens, expert_ids.T, gate_weights.T,
        up_weight, up_bias, down_weight, down_bias,
    )
    return attn_out.T, moe_out


def solution(mesh):
    in_specs = (
        P(("groups", "seq"), ("exp", "tp")),
        P(("groups", "seq"), ("exp", "tp")),
        P(("groups", "seq"), ("exp", "tp")),
        P(("groups", "seq"), ("exp", "tp")),
        P(("groups", "seq"), ("exp", "tp")),
        P(("groups", "seq")),
        P(("groups", "seq", "exp", "tp"), None),
        P(("groups", "seq", "exp", "tp"), None),
        P(("groups", "seq", "exp", "tp"), None),
        P("seq", None, ("exp", "tp")),
        P("seq", ("exp", "tp")),
        P("seq", ("exp", "tp"), None),
        P("seq", None),
    )
    out_specs = (P(("groups", "seq"), ("exp", "tp")), P(("groups", "seq", "exp", "tp"), None))
    return jax.shard_map(local, mesh=mesh, in_specs=in_specs, out_specs=out_specs, check_vma=False)
```

profile of v0, /device:TPU:0, one launch (start us, length us, event | category | flops | bytes accessed | tf_op | source)
XLA Modules:
  0.0 68.6 jit_solution(16999512713926828568)
XLA Ops:
  0.6 64.6 %shard_map.140 = (bf16[288,256]{1,0:T(8,128)(2,1)}, bf16[128,1152]{1,0:T(8,128)(2,1)}) custom-call(bf16[288,256]{1,0:T(8,128)(2,1)} %bitcast.9, bf16[288,256]{1,0:T(8,128)(2,1)} %bitcast.10, bf16[288,256]{1,0:T(8,128)(2,1)} %bitcast.11, bf16[288,256]{1,0:T(8,128)(2,1)} %bitcast.12, bf16[288,256]{1,0:T(8,128)(2,1)} %bitcast.13, s32[2]{0:T(128)} %flags.1, ...), custom_call_target="tpu_custom_call" | custom-call | tf_op jit(solution)/shard_map/pallas_call | solution.py:316
  65.3 1.6 %copy.17 = bf16[256,288]{0,1:T(8,128)(2,1)} copy(bf16[256,288]{0,1:T(8,128)(2,1)} %bitcast.8) | data formatting | bytes 294912
  66.9 1.7 %copy.18 = bf16[128,1152]{1,0:T(8,128)(2,1)} copy(bf16[128,1152]{1,0:T(8,128)(2,1)} %get-tuple-element.9) | data formatting | bytes 589824
where the time goes:
time: 68.8 us; the launch traced here: 68.6 us
  Pallas kernels  64.6 us (94%)
  local copies, waits for them, and re-layouts  3.28 us (5%)
    pallas_call x1, Pallas kernels, local(): pl.pallas_call(functools.partial(layer_kernel, (S, X, capp)), out_shape=(...  64.6 us
    unnamed x2, local copies, waits for them, and re-layouts  3.28 us

commit v1 on v0

--- a/solution.py
+++ b/solution.py
@@ -12,6 +12,7 @@
 MESH = pl.DeviceIdType.MESH
 F32 = jnp.float32
 BF16 = jnp.bfloat16
+VMEM_LIMIT = 40 * 1024 * 1024
 
 
 def layer_kernel(
@@ -298,6 +299,341 @@
     lax.fori_loop(0, S, drain_chunk, jnp.int32(0))
 
 
+def fast_kernel(
+    sizes,
+    q_hbm, fk_hbm, fv_hbm, sk_hbm, sv_hbm, flags_hbm, tok_hbm, ids_hbm, gate_hbm,
+    up_hbm, upb_hbm, down_hbm, downb_hbm,
+    attn_ref, moe_ref,
+    q_v, fresh_k, fresh_v, stale_k, stale_v, flags, tok_v, ids_v, gate_v,
+    up_v, upb_v, down_v, downb_v,
+    disp, rows, outs, tpin, xin, fin, ret, kv, keys_v, acc, moe, turn,
+    in_sem,
+    z_send, z_recv, xf_send, xf_recv, tf_send, tf_recv,
+    tr_send, tr_recv, xr_send, xr_recv, zr_send, zr_recv, kv_right, kv_left, kv_recv,
+):
+    S, X, capp = sizes
+    s, x, c = lax.axis_index("seq"), lax.axis_index("exp"), lax.axis_index("tp")
+    oc, ox = 1 - c, 1 - x
+    T, D = tok_v.shape
+    W, L = q_v.shape
+    heads = W // HD
+    blocks = flags.shape[0]
+    blk = L // blocks
+
+    barrier = pltpu.get_barrier_semaphore()
+    for i in range(1, S):
+        pl.semaphore_signal(barrier, inc=1, device_id={"seq": lax.rem(s + i, S)}, device_id_type=MESH)
+    pl.semaphore_signal(barrier, inc=1, device_id={"exp": ox}, device_id_type=MESH)
+    pl.semaphore_signal(barrier, inc=1, device_id={"tp": oc}, device_id_type=MESH)
+
+    pairs = (
+        (ids_hbm, ids_v), (tok_hbm, tok_v), (flags_hbm, flags),
+        (fk_hbm, fresh_k), (sk_hbm, stale_k), (fv_hbm, fresh_v), (sv_hbm, stale_v),
+        (up_hbm.at[0], up_v), (upb_hbm, upb_v), (down_hbm.at[0], down_v), (downb_hbm, downb_v),
+        (q_hbm, q_v), (gate_hbm, gate_v),
+    )
+    loads = [pltpu.make_async_copy(a, b, in_sem.at[i]) for i, (a, b) in enumerate(pairs)]
+    for load in loads:
+        load.start()
+
+    def rdma(src, dst, ssem, rsem, where):
+        return pltpu.make_async_remote_copy(
+            src_ref=src, dst_ref=dst, send_sem=ssem, recv_sem=rsem,
+            device_id=where, device_id_type=MESH,
+        )
+
+    def z_copy(e, slot):
+        return rdma(disp.at[e], rows.at[slot, x, c], z_send.at[e], z_recv.at[slot], {"seq": e})
+
+    def x_forward(src, origin):
+        return rdma(
+            rows.at[src, origin, c], rows.at[src, origin, c],
+            xf_send.at[src], xf_recv.at[src], {"exp": ox},
+        )
+
+    def t_forward(src, origin, side):
+        return rdma(
+            rows.at[src, origin, side], rows.at[src, origin, side],
+            tf_send.at[src, origin], tf_recv.at[src, origin], {"tp": oc},
+        )
+
+    def t_reduce(src, origin):
+        return rdma(
+            outs.at[src, origin, oc], tpin.at[src, origin],
+            tr_send.at[src, origin], tr_recv.at[src, origin], {"tp": oc},
+        )
+
+    def x_reduce(src):
+        return rdma(outs.at[src, ox, c], xin.at[src], xr_send.at[src], xr_recv.at[src], {"exp": ox})
+
+    def z_return(src, slot):
+        return rdma(fin.at[src], ret.at[slot], zr_send.at[src], zr_recv.at[slot], {"seq": src})
+
+    def kv_copy(b, part, step):
+        sems = kv_right if step > 0 else kv_left
+        return rdma(
+            kv.at[b, part], kv.at[b, part], sems.at[b, part], kv_recv.at[b, part], {"seq": s + step}
+        )
+
+    def mirrored(end, inner):
+        near = jnp.where((s == 0) | (s == S - 1), end, inner)
+        return jnp.where(2 * s < S, near, S - 1 - near)
+
+    targets = [mirrored(a, b) for a, b in ((S - 1, 2), (1, 0), (2, S - 1))]
+    order = [s] + [mirrored(a, b) for a, b in ((1, 2), (S - 1, 0), (2, S - 1))]
+
+    loads[0].wait()
+    loads[1].wait()
+    expert = lax.broadcasted_iota(jnp.int32, (S, T), 0)
+    named = (ids_v[0:1, :] == expert) | (ids_v[1:2, :] == expert)
+    earlier = lax.broadcasted_iota(jnp.int32, (T, T), 0) < lax.broadcasted_iota(jnp.int32, (T, T), 1)
+    place = jnp.dot(
+        jnp.where(named, 1.0, 0.0).astype(BF16),
+        jnp.where(earlier, 1.0, 0.0).astype(BF16),
+        preferred_element_type=F32,
+    )
+    slotted = jnp.where(named, place, -1.0)
+    slot_rows = lax.broadcasted_iota(jnp.int32, (capp, T), 0).astype(F32)
+    for e in range(S):
+        pick = jnp.where(slotted[e : e + 1, :] == slot_rows, 1.0, 0.0).astype(BF16)
+        disp[e] = jnp.dot(pick, tok_v[...], preferred_element_type=F32).astype(BF16)
+    rows[s, x, c] = disp[s]
+    for load in loads[2:7]:
+        load.wait()
+    for b in range(blocks):
+        fresh = flags[b] == 1
+        part = pl.ds(b * blk, blk)
+        kv[s, 0, :, part] = jnp.where(fresh, fresh_k[:, part], stale_k[:, part])
+        kv[s, 1, :, part] = jnp.where(fresh, fresh_v[:, part], stale_v[:, part])
+
+    pl.semaphore_wait(barrier, S - 1 + 1 + 1)
+
+    def forward(src):
+        x_forward(src, x).start()
+        t_forward(src, x, c).start()
+
+    def arrive(src):
+        z_copy(src, src).wait_recv()
+        forward(src)
+
+    for e in targets:
+        z_copy(e, s).start()
+    forward(s)
+
+    def relay(step, part):
+        low, high = s - (step - 1), s + (step - 1)
+
+        @pl.when(low >= 0)
+        def _():
+            @pl.when(low < s)
+            def _():
+                kv_copy(low, part, 1).wait_recv()
+
+            @pl.when(s + 1 < S)
+            def _():
+                kv_copy(low, part, 1).start()
+
+        @pl.when(high < S)
+        def _():
+            @pl.when(high > s)
+            def _():
+                kv_copy(high, part, -1).wait_recv()
+
+            @pl.when(s - 1 >= 0)
+            def _():
+                kv_copy(high, part, -1).start()
+
+    relay(1, 0)
+    relay(1, 1)
+    for load in loads[7:]:
+        load.wait()
+
+    def mlp(src, origin):
+        block = rows[src, origin].reshape(2 * capp, D)
+        hidden = jnp.dot(block, up_v[...], preferred_element_type=F32) + upb_v[...]
+        hidden = jax.nn.gelu(hidden).astype(BF16)
+        result = jnp.dot(hidden, down_v[...], preferred_element_type=F32).astype(BF16)
+        outs[src, origin] = result.reshape(2, capp, D)
+        t_reduce(src, origin).start()
+
+    def mine(src):
+        t_forward(src, x, oc).wait_recv()
+        mlp(src, x)
+
+    def crossed(src):
+        x_forward(src, ox).wait_recv()
+        t_forward(src, ox, c).start()
+
+    def other(src):
+        t_forward(src, ox, oc).wait_recv()
+        mlp(src, ox)
+
+    def reduce(src):
+        t_reduce(src, ox).wait_recv()
+        outs[src, ox, c] = (outs[src, ox, c].astype(F32) + tpin[src, ox].astype(F32)).astype(BF16)
+        x_reduce(src).start()
+
+    def finish(src):
+        t_reduce(src, x).wait_recv()
+        total = outs[src, x, c].astype(F32) + tpin[src, x].astype(F32) + downb_v[...]
+        x_reduce(src).wait_recv()
+        return (total + xin[src].astype(F32)).astype(BF16)
+
+    def finish_send(src):
+        fin[src] = finish(src)
+        z_return(src, s).start()
+
+    o0, o1, o2, o3 = order
+    mine(o0)
+    turn[...] = jnp.zeros_like(turn)
+    for i, e in enumerate(order):
+        hit = [ids_v[j : j + 1, :] == e for j in range(2)]
+        spot = jnp.sum(jnp.where(expert == e, place, 0.0), axis=0, keepdims=True)
+        turn[i : i + 1, :] = jnp.where(hit[0] | hit[1], spot, -1.0)
+        turn[S + i : S + i + 1, :] = sum(
+            jnp.where(hit[j], gate_v[j : j + 1, :], 0.0) for j in range(2)
+        )
+    turned = turn[...].T
+    slot_lane = lax.broadcasted_iota(jnp.int32, (T, capp), 1).astype(F32)
+    arrive(o1)
+    crossed(o0)
+    mine(o1)
+    other(o0)
+    arrive(o2)
+    mine(o2)
+    crossed(o1)
+    arrive(o3)
+    other(o1)
+    mine(o3)
+    reduce(o1)
+    crossed(o2)
+    other(o2)
+    relay(2, 0)
+    reduce(o2)
+    relay(2, 1)
+    crossed(o3)
+    other(o3)
+    reduce(o3)
+    reduce(o0)
+    relay(3, 0)
+    finish_send(o1)
+    relay(3, 1)
+    finish_send(o2)
+    finish_send(o3)
+    relay(4, 0)
+    relay(4, 1)
+
+    for i in range(S):
+        keys_v[pl.ds(i * L, L), :] = kv[i, 0].T
+    scale = 1.0 / math.sqrt(HD)
+    channel = lax.broadcasted_iota(jnp.int32, (W, L), 0)
+
+    def head(h, unused):
+        mask = (channel >= h * HD) & (channel < (h + 1) * HD)
+        query = jnp.where(mask, q_v[...].astype(F32), 0.0).astype(BF16)
+        scores = jnp.dot(keys_v[...], query, preferred_element_type=F32) * scale
+        probs = jnp.exp(scores - jnp.max(scores, axis=0, keepdims=True))
+        total = jnp.sum(probs, axis=0, keepdims=True)
+        weights = probs.astype(BF16)
+        mixed = jnp.zeros((W, L), F32)
+        for i in range(S):
+            mixed += jnp.dot(kv[i, 1], weights[i * L : (i + 1) * L], preferred_element_type=F32)
+        acc[...] = jnp.where(mask, mixed / total, acc[...])
+        return unused
+
+    acc[...] = jnp.zeros_like(acc)
+    lax.fori_loop(0, heads, head, jnp.int32(0))
+    attn_ref[...] = acc[...].astype(BF16)
+
+    def combine(i, values):
+        pick = jnp.where(turned[:, i : i + 1] == slot_lane, 1.0, 0.0).astype(BF16)
+        return jnp.dot(pick, values, preferred_element_type=F32) * turned[:, S + i : S + i + 1]
+
+    moe[...] = combine(0, finish(s))
+    for i in range(1, S - 1):
+        z_return(s, order[i]).wait_recv()
+        moe[...] += combine(i, ret[order[i]])
+    z_return(s, order[S - 1]).wait_recv()
+    moe_ref[...] = (moe[...] + combine(S - 1, ret[order[S - 1]])).astype(BF16)
+
+    def drain(i, unused):
+        to = lax.rem(s + i, S)
+        z_copy(to, s).wait_send()
+        z_return(to, s).wait_send()
+        return unused
+
+    lax.fori_loop(1, S, drain, jnp.int32(0))
+
+    def drain_chunk(i, unused):
+        x_forward(i, x).wait_send()
+        x_reduce(i).wait_send()
+        for origin in range(X):
+            t_forward(i, origin, c).wait_send()
+            t_reduce(i, origin).wait_send()
+        for part in range(2):
+
+            @pl.when((i <= s) & (s + 1 < S))
+            def _():
+                kv_copy(i, part, 1).wait_send()
+
+            @pl.when((i >= s) & (s - 1 >= 0))
+            def _():
+                kv_copy(i, part, -1).wait_send()
+
+        return unused
+
+    lax.fori_loop(0, S, drain_chunk, jnp.int32(0))
+
+
+def fast_call(S, X, capp, args):
+    q, tok, up, flags = args[0], args[6], args[9], args[5]
+    width, length = q.shape
+    tokens, D = tok.shape
+    hidden = up.shape[2]
+    hbm = pl.BlockSpec(memory_space=pltpu.HBM)
+    vmem = pl.BlockSpec(memory_space=pltpu.VMEM)
+    dma = pltpu.SemaphoreType.DMA
+    half = pltpu.VMEM((width, length), BF16)
+    slots = pltpu.VMEM((S, capp, D), BF16)
+    return pl.pallas_call(
+        functools.partial(fast_kernel, (S, X, capp)),
+        out_shape=(
+            jax.ShapeDtypeStruct((width, length), BF16),
+            jax.ShapeDtypeStruct((tokens, D), BF16),
+        ),
+        in_specs=[hbm] * 13,
+        out_specs=(vmem, vmem),
+        scratch_shapes=[
+            half, half, half, half, half,
+            pltpu.SMEM(flags.shape, jnp.int32),
+            pltpu.VMEM((tokens, D), BF16),
+            pltpu.VMEM((2, tokens), jnp.int32),
+            pltpu.VMEM((2, tokens), F32),
+            pltpu.VMEM((D, hidden), BF16),
+            pltpu.VMEM((1, hidden), F32),
+            pltpu.VMEM((hidden, D), BF16),
+            pltpu.VMEM((1, D), F32),
+            slots,
+            pltpu.VMEM((S, X, 2, capp, D), BF16),
+            pltpu.VMEM((S, X, 2, capp, D), BF16),
+            pltpu.VMEM((S, X, capp, D), BF16),
+            slots, slots, slots,
+            pltpu.VMEM((S, 2, width, length), BF16),
+            pltpu.VMEM((S * length, width), BF16),
+            pltpu.VMEM((width, length), F32),
+            pltpu.VMEM((tokens, D), F32),
+            pltpu.VMEM((128, tokens), F32),
+            dma((13,)),
+            dma((S,)), dma((S,)), dma((S,)), dma((S,)), dma((S, X)), dma((S, X)),
+            dma((S, X)), dma((S, X)), dma((S,)), dma((S,)), dma((S,)), dma((S,)),
+            dma((S, 2)), dma((S, 2)), dma((S, 2)),
+        ],
+        compiler_params=pltpu.CompilerParams(
+            collective_id=0, has_side_effects=True, vmem_limit_bytes=VMEM_LIMIT
+        ),
+    )(*[pltpu.with_memory_space_constraint(a, pltpu.HBM) for a in args])
+
+
 def local(
     attn_query, fresh_keys, fresh_values, stale_keys, stale_values, block_flags,
     moe_tokens, expert_ids, gate_weights, up_weight, up_bias, down_weight, down_bias,
@@ -309,6 +645,13 @@
     hidden = up_weight.shape[2]
     cap = 5 * tokens // (2 * S)
     capp = -(-cap // 16) * 16
+    if (S, X) == (4, 2):
+        attn_out, moe_out = fast_call(S, X, capp, (
+            attn_query.T, fresh_keys.T, fresh_values.T, stale_keys.T, stale_values.T, block_flags,
+            moe_tokens, expert_ids.T, gate_weights.T,
+            up_weight, up_bias, down_weight, down_bias,
+        ))
+        return attn_out.T, moe_out
     vmem = pl.BlockSpec(memory_space=pltpu.VMEM)
     smem = pl.BlockSpec(memory_space=pltpu.SMEM)
     hbm = pl.BlockSpec(memory_space=pl.ANY)

time: 68.8 us -> 59 us (0.86)
  Pallas kernels: 64.6 us -> 56.8 us
  local copies, waits for them, and re-layouts: 3.28 us -> 1.38 us
    pallas_call x1, Pallas kernels: 64.6 us -> 56.8 us  [fast_call(): pl.pallas_call(functools.partial(fast_kernel, (S, X, capp)), out_shape=(j...]
    unnamed x2, local copies, waits for them, and re-layouts: 3.28 us -> 1.38 us
where the time goes in v1:
time: 59 us; the launch traced here: 58.8 us
  Pallas kernels  56.8 us (96%)
  local copies, waits for them, and re-layouts  1.38 us (2%)
  between operations  0.64 us (1%)
    pallas_call x1, Pallas kernels, fast_call(): pl.pallas_call(functools.partial(fast_kernel, (S, X, capp)), out_shape=(j...  56.8 us
    unnamed x2, local copies, waits for them, and re-layouts  1.38 us

profile of v1, /device:TPU:0, one launch (start us, length us, event | category | flops | bytes accessed | tf_op | source)
XLA Modules:
  0.0 58.8 jit_solution(2858116140793296799)
XLA Ops:
  0.6 56.8 %shard_map.140 = (bf16[288,256]{1,0:T(8,128)(2,1)S(1)}, bf16[128,1152]{1,0:T(8,128)(2,1)S(1)}) custom-call(bf16[288,256]{1,0:T(8,128)(2,1)} %bitcast.9, bf16[288,256]{1,0:T(8,128)(2,1)} %bitcast.10, bf16[288,256]{1,0:T(8,128)(2,1)} %bitcast.11, bf16[288,256]{1,0:T(8,128)(2,1)} %bitcast.12, bf16[288,256]{1,0:T(8,128)(2,1)} %bitcast.13, s32[2]{0:T(128)} %flags_hbm.1, ...), custom_call_target="tpu_custom_call" | custom-call | tf_op jit(solution)/shard_map/pallas_call | solution.py:598
  57.4 0.7 %copy.17 = bf16[256,288]{0,1:T(8,128)(2,1)} copy(bf16[256,288]{0,1:T(8,128)(2,1)S(1)} %bitcast.8) | data formatting | bytes 294912
  58.1 0.7 %copy.18 = bf16[128,1152]{1,0:T(8,128)(2,1)} copy(bf16[128,1152]{1,0:T(8,128)(2,1)S(1)} %get-tuple-element.9) | data formatting | bytes 589824

commit v2 on v1

--- a/solution.py
+++ b/solution.py
@@ -306,10 +306,10 @@
     attn_ref, moe_ref,
     q_v, fresh_k, fresh_v, stale_k, stale_v, flags, tok_v, ids_v, gate_v,
     up_v, upb_v, down_v, downb_v,
-    disp, rows, outs, tpin, xin, fin, ret, kv, keys_v, acc, moe, turn,
+    disp, rows, outs, tpin, xin, fin, ret, kv, keys_v, q_in, o_out, o_in, masked, acc, stat, moe, turn,
     in_sem,
     z_send, z_recv, xf_send, xf_recv, tf_send, tf_recv,
-    tr_send, tr_recv, xr_send, xr_recv, zr_send, zr_recv, kv_right, kv_left, kv_recv,
+    tr_send, tr_recv, xr_send, xr_recv, zr_send, zr_recv, kv_send, kv_recv, qo_send, qo_recv,
 ):
     S, X, capp = sizes
     s, x, c = lax.axis_index("seq"), lax.axis_index("exp"), lax.axis_index("tp")
@@ -369,18 +369,25 @@
     def z_return(src, slot):
         return rdma(fin.at[src], ret.at[slot], zr_send.at[src], zr_recv.at[slot], {"seq": src})
 
-    def kv_copy(b, part, step):
-        sems = kv_right if step > 0 else kv_left
-        return rdma(
-            kv.at[b, part], kv.at[b, part], sems.at[b, part], kv_recv.at[b, part], {"seq": s + step}
-        )
+    mate, facing = s + 1 - 2 * lax.rem(s, 2), S - 1 - s
+    far = S - 1 - mate
+    inner = (s != 0) & (s != S - 1)
+
+    def kv_copy(b, part, to):
+        return rdma(kv.at[b, part], kv.at[b, part], kv_send.at[b, part], kv_recv.at[b, part], {"seq": to})
+
+    def q_copy():
+        return rdma(q_v, q_in, qo_send.at[0], qo_recv.at[0], {"seq": mate})
+
+    def o_copy():
+        return rdma(o_out, o_in, qo_send.at[1], qo_recv.at[1], {"seq": mate})
 
     def mirrored(end, inner):
         near = jnp.where((s == 0) | (s == S - 1), end, inner)
         return jnp.where(2 * s < S, near, S - 1 - near)
 
-    targets = [mirrored(a, b) for a, b in ((S - 1, 2), (1, 0), (2, S - 1))]
-    order = [s] + [mirrored(a, b) for a, b in ((1, 2), (S - 1, 0), (2, S - 1))]
+    targets = [mirrored(a, b) for a, b in ((1, 2), (S - 1, 0), (2, S - 1))]
+    order = [s, mate, facing, far]
 
     loads[0].wait()
     loads[1].wait()
@@ -420,33 +427,55 @@
         z_copy(e, s).start()
     forward(s)
 
-    def relay(step, part):
-        low, high = s - (step - 1), s + (step - 1)
-
-        @pl.when(low >= 0)
-        def _():
-            @pl.when(low < s)
-            def _():
-                kv_copy(low, part, 1).wait_recv()
-
-            @pl.when(s + 1 < S)
-            def _():
-                kv_copy(low, part, 1).start()
-
-        @pl.when(high < S)
-        def _():
-            @pl.when(high > s)
-            def _():
-                kv_copy(high, part, -1).wait_recv()
-
-            @pl.when(s - 1 >= 0)
-            def _():
-                kv_copy(high, part, -1).start()
-
-    relay(1, 0)
-    relay(1, 1)
+    onward = jnp.where(inner, facing, mate)
+    kv_copy(s, 0, onward).start()
+    kv_copy(s, 1, onward).start()
+
     for load in loads[7:]:
         load.wait()
+
+    @pl.when(jnp.logical_not(inner))
+    def _():
+        q_copy().start()
+
+    scale = 1.0 / math.sqrt(HD)
+    channel = lax.broadcasted_iota(jnp.int32, (W, L), 0)
+
+    def ask(i, source):
+        for h in range(heads):
+            own = (channel >= h * HD) & (channel < (h + 1) * HD)
+            masked[i, h] = jnp.where(own, source[...].astype(F32), 0.0).astype(BF16)
+
+    def take(b):
+        keys_v[b] = kv[b, 0].T
+
+    def attend(i, b, first=False):
+        for h in range(heads):
+            lo, hi = h * HD, (h + 1) * HD
+            a, z = lo // 128 * 128, min(-(-hi // 128) * 128, W)
+            scores = jnp.dot(keys_v[b, :, a:z], masked[i, h, a:z, :], preferred_element_type=F32) * scale
+            top = jnp.max(scores, axis=0, keepdims=True)
+            if not first:
+                before = stat[i, h : h + 1, :]
+                top = jnp.maximum(before, top)
+                fade = jnp.exp(before - top)
+            probs = jnp.exp(scores - top)
+            total = jnp.sum(probs, axis=0, keepdims=True)
+            a, z = lo // 16 * 16, -(-hi // 16) * 16
+            mixed = jnp.dot(kv[b, 1, a:z, :], probs.astype(BF16), preferred_element_type=F32)
+            mixed = mixed[lo - a : hi - a]
+            if not first:
+                total = stat[i, heads + h : heads + h + 1, :] * fade + total
+                mixed = acc[i, lo:hi, :] * fade + mixed
+            stat[i, h : h + 1, :] = top
+            stat[i, heads + h : heads + h + 1, :] = total
+            acc[i, lo:hi, :] = mixed
+
+    def answer(i):
+        for h in range(heads):
+            lo, hi = h * HD, (h + 1) * HD
+            acc[i, lo:hi, :] = acc[i, lo:hi, :] / stat[i, heads + h : heads + h + 1, :]
+        return acc[i].astype(BF16)
 
     def mlp(src, origin):
         block = rows[src, origin].reshape(2 * capp, D)
@@ -495,55 +524,103 @@
         )
     turned = turn[...].T
     slot_lane = lax.broadcasted_iota(jnp.int32, (T, capp), 1).astype(F32)
+
+    outer = jnp.logical_not(inner)
+    r1, r2, r3 = (jnp.where(inner, a, b) for a, b in ((o1, o2), (o2, o3), (o3, o1)))
+
+    @pl.when(inner)
+    def _():
+        ask(0, q_v)
+        take(s)
+        attend(0, s, first=True)
+
     arrive(o1)
+
+    @pl.when(inner)
+    def _():
+        arrive(o2)
+
     crossed(o0)
     mine(o1)
     other(o0)
-    arrive(o2)
+    crossed(o1)
+
+    @pl.when(outer)
+    def _():
+        arrive(o2)
+
+    other(o1)
     mine(o2)
-    crossed(o1)
-    arrive(o3)
-    other(o1)
+
+    @pl.when(outer)
+    def _():
+        arrive(o3)
+
+    crossed(o2)
+
+    @pl.when(inner)
+    def _():
+        arrive(o3)
+        reduce(o1)
+        kv_copy(mate, 0, mate).wait_recv()
+        kv_copy(mate, 0, facing).start()
+
+    other(o2)
     mine(o3)
-    reduce(o1)
-    crossed(o2)
-    other(o2)
-    relay(2, 0)
     reduce(o2)
-    relay(2, 1)
+
+    @pl.when(inner)
+    def _():
+        kv_copy(mate, 1, mate).wait_recv()
+        kv_copy(mate, 1, facing).start()
+        take(mate)
+
     crossed(o3)
+
+    @pl.when(inner)
+    def _():
+        attend(0, mate)
+
     other(o3)
+
+    @pl.when(inner)
+    def _():
+        q_copy().wait_recv()
+        ask(1, q_in)
+        attend(1, s, first=True)
+
     reduce(o3)
+
+    @pl.when(outer)
+    def _():
+        reduce(o1)
+
     reduce(o0)
-    relay(3, 0)
-    finish_send(o1)
-    relay(3, 1)
-    finish_send(o2)
-    finish_send(o3)
-    relay(4, 0)
-    relay(4, 1)
-
-    for i in range(S):
-        keys_v[pl.ds(i * L, L), :] = kv[i, 0].T
-    scale = 1.0 / math.sqrt(HD)
-    channel = lax.broadcasted_iota(jnp.int32, (W, L), 0)
-
-    def head(h, unused):
-        mask = (channel >= h * HD) & (channel < (h + 1) * HD)
-        query = jnp.where(mask, q_v[...].astype(F32), 0.0).astype(BF16)
-        scores = jnp.dot(keys_v[...], query, preferred_element_type=F32) * scale
-        probs = jnp.exp(scores - jnp.max(scores, axis=0, keepdims=True))
-        total = jnp.sum(probs, axis=0, keepdims=True)
-        weights = probs.astype(BF16)
-        mixed = jnp.zeros((W, L), F32)
-        for i in range(S):
-            mixed += jnp.dot(kv[i, 1], weights[i * L : (i + 1) * L], preferred_element_type=F32)
-        acc[...] = jnp.where(mask, mixed / total, acc[...])
-        return unused
-
-    acc[...] = jnp.zeros_like(acc)
-    lax.fori_loop(0, heads, head, jnp.int32(0))
-    attn_ref[...] = acc[...].astype(BF16)
+    finish_send(r1)
+
+    @pl.when(inner)
+    def _():
+        attend(1, mate)
+        kv_copy(facing, 0, facing).wait_recv()
+        kv_copy(facing, 1, facing).wait_recv()
+        take(facing)
+        attend(1, facing)
+        attend(0, facing)
+
+    finish_send(r2)
+
+    @pl.when(inner)
+    def _():
+        kv_copy(far, 0, facing).wait_recv()
+        kv_copy(far, 1, facing).wait_recv()
+        take(far)
+        attend(1, far)
+        o_out[...] = answer(1)
+        o_copy().start()
+        attend(0, far)
+        attn_ref[...] = answer(0)
+
+    finish_send(r3)
 
     def combine(i, values):
         pick = jnp.where(turned[:, i : i + 1] == slot_lane, 1.0, 0.0).astype(BF16)
@@ -553,6 +630,12 @@
     for i in range(1, S - 1):
         z_return(s, order[i]).wait_recv()
         moe[...] += combine(i, ret[order[i]])
+
+    @pl.when(jnp.logical_not(inner))
+    def _():
+        o_copy().wait_recv()
+        attn_ref[...] = o_in[...]
+
     z_return(s, order[S - 1]).wait_recv()
     moe_ref[...] = (moe[...] + combine(S - 1, ret[order[S - 1]])).astype(BF16)
 
@@ -570,19 +653,21 @@
         for origin in range(X):
             t_forward(i, origin, c).wait_send()
             t_reduce(i, origin).wait_send()
+        return unused
+
+    lax.fori_loop(0, S, drain_chunk, jnp.int32(0))
+    for part in range(2):
+        kv_copy(s, part, onward).wait_send()
+
+    @pl.when(inner)
+    def _():
         for part in range(2):
-
-            @pl.when((i <= s) & (s + 1 < S))
-            def _():
-                kv_copy(i, part, 1).wait_send()
-
-            @pl.when((i >= s) & (s - 1 >= 0))
-            def _():
-                kv_copy(i, part, -1).wait_send()
-
-        return unused
-
-    lax.fori_loop(0, S, drain_chunk, jnp.int32(0))
+            kv_copy(mate, part, facing).wait_send()
+        o_copy().wait_send()
+
+    @pl.when(jnp.logical_not(inner))
+    def _():
+        q_copy().wait_send()
 
 
 def fast_call(S, X, capp, args):
@@ -619,14 +704,17 @@
             pltpu.VMEM((S, X, capp, D), BF16),
             slots, slots, slots,
             pltpu.VMEM((S, 2, width, length), BF16),
-            pltpu.VMEM((S * length, width), BF16),
-            pltpu.VMEM((width, length), F32),
+            pltpu.VMEM((S, length, width), BF16),
+            half, half, half,
+            pltpu.VMEM((2, width // HD, width, length), BF16),
+            pltpu.VMEM((2, width, length), F32),
+            pltpu.VMEM((2, 2 * width // HD, length), F32),
             pltpu.VMEM((tokens, D), F32),
             pltpu.VMEM((128, tokens), F32),
             dma((13,)),
             dma((S,)), dma((S,)), dma((S,)), dma((S,)), dma((S, X)), dma((S, X)),
             dma((S, X)), dma((S, X)), dma((S,)), dma((S,)), dma((S,)), dma((S,)),
-            dma((S, 2)), dma((S, 2)), dma((S, 2)),
+            dma((S, 2)), dma((S, 2)), dma((2,)), dma((2,)),
         ],
         compiler_params=pltpu.CompilerParams(
             collective_id=0, has_side_effects=True, vmem_limit_bytes=VMEM_LIMIT

time: 59 us -> 56.2 us (0.953)
  Pallas kernels: 56.8 us -> 54.1 us
    pallas_call x1, Pallas kernels: 56.8 us -> 54.1 us  [fast_call(): pl.pallas_call(functools.partial(fast_kernel, (S, X, capp)), out_shape=(j...]
where the time goes in v2:
time: 56.2 us; the launch traced here: 56.1 us
  Pallas kernels  54.1 us (96%)
  local copies, waits for them, and re-layouts  1.38 us (2%)
  between operations  0.64 us (1%)
    pallas_call x1, Pallas kernels, fast_call(): pl.pallas_call(functools.partial(fast_kernel, (S, X, capp)), out_shape=(j...  54.1 us
    unnamed x2, local copies, waits for them, and re-layouts  1.38 us

profile of v2, /device:TPU:0, one launch (start us, length us, event | category | flops | bytes accessed | tf_op | source)
XLA Modules:
  0.0 56.1 jit_solution(18078186038550966560)
XLA Ops:
  0.6 54.1 %shard_map.140 = (bf16[288,256]{1,0:T(8,128)(2,1)S(1)}, bf16[128,1152]{1,0:T(8,128)(2,1)S(1)}) custom-call(bf16[288,256]{1,0:T(8,128)(2,1)} %bitcast.9, bf16[288,256]{1,0:T(8,128)(2,1)} %bitcast.10, bf16[288,256]{1,0:T(8,128)(2,1)} %bitcast.11, bf16[288,256]{1,0:T(8,128)(2,1)} %bitcast.12, bf16[288,256]{1,0:T(8,128)(2,1)} %bitcast.13, s32[2]{0:T(128)} %flags_hbm.1, ...), custom_call_target="tpu_custom_call" | custom-call | tf_op jit(solution)/shard_map/pallas_call | solution.py:683
  54.7 0.7 %copy.17 = bf16[256,288]{0,1:T(8,128)(2,1)} copy(bf16[256,288]{0,1:T(8,128)(2,1)S(1)} %bitcast.8) | data formatting | bytes 294912
  55.4 0.7 %copy.18 = bf16[128,1152]{1,0:T(8,128)(2,1)} copy(bf16[128,1152]{1,0:T(8,128)(2,1)S(1)} %get-tuple-element.9) | data formatting | bytes 589824

commit v3 on v2

--- a/solution.py
+++ b/solution.py
@@ -526,7 +526,7 @@
     slot_lane = lax.broadcasted_iota(jnp.int32, (T, capp), 1).astype(F32)
 
     outer = jnp.logical_not(inner)
-    r1, r2, r3 = (jnp.where(inner, a, b) for a, b in ((o1, o2), (o2, o3), (o3, o1)))
+    r1, r3 = jnp.where(inner, o1, o2), jnp.where(inner, o3, o1)
 
     @pl.when(inner)
     def _():
@@ -607,7 +607,9 @@
         attend(1, facing)
         attend(0, facing)
 
-    finish_send(r2)
+    @pl.when(outer)
+    def _():
+        finish_send(o3)
 
     @pl.when(inner)
     def _():
@@ -622,6 +624,10 @@
 
     finish_send(r3)
 
+    @pl.when(inner)
+    def _():
+        finish_send(o2)
+
     def combine(i, values):
         pick = jnp.where(turned[:, i : i + 1] == slot_lane, 1.0, 0.0).astype(BF16)
         return jnp.dot(pick, values, preferred_element_type=F32) * turned[:, S + i : S + i + 1]
@@ -668,6 +674,30 @@
     @pl.when(jnp.logical_not(inner))
     def _():
         q_copy().wait_send()
+
+
+def store_kernel(attn_ref, moe_ref, attn_hbm, moe_hbm, sems):
+    stores = [
+        pltpu.make_async_copy(attn_ref, attn_hbm, sems.at[0]),
+        pltpu.make_async_copy(moe_ref, moe_hbm, sems.at[1]),
+    ]
+    for store in stores:
+        store.start()
+    for store in stores:
+        store.wait()
+
+
+def store(attn, moe):
+    vmem = pl.BlockSpec(memory_space=pltpu.VMEM)
+    hbm = pl.BlockSpec(memory_space=pltpu.HBM)
+    return pl.pallas_call(
+        store_kernel,
+        out_shape=tuple(jax.ShapeDtypeStruct(a.shape, a.dtype) for a in (attn, moe)),
+        in_specs=[vmem, vmem],
+        out_specs=(hbm, hbm),
+        scratch_shapes=[pltpu.SemaphoreType.DMA((2,))],
+        compiler_params=pltpu.CompilerParams(vmem_limit_bytes=VMEM_LIMIT // 8),
+    )(attn, moe)
 
 
 def fast_call(S, X, capp, args):
@@ -739,6 +769,7 @@
             moe_tokens, expert_ids.T, gate_weights.T,
             up_weight, up_bias, down_weight, down_bias,
         ))
+        attn_out, moe_out = store(attn_out, moe_out)
         return attn_out.T, moe_out
     vmem = pl.BlockSpec(memory_space=pltpu.VMEM)
     smem = pl.BlockSpec(memory_space=pltpu.SMEM)

time: 56.2 us -> 53.8 us (0.957)
  local copies, waits for them, and re-layouts: 1.38 us -> 0 us
  Pallas kernels: 54.1 us -> 52.8 us
    pallas_call x1, Pallas kernels: 54.1 us -> 52 us  [fast_call(): pl.pallas_call(functools.partial(fast_kernel, (S, X, capp)), out_shape=(j...]
    unnamed x2 -> x0, local copies, waits for them, and re-layouts: 1.38 us -> none
    pallas_call x0 -> x1, Pallas kernels: none -> 0.78 us  [store(): pl.pallas_call(store_kernel, out_shape=tuple((jax.ShapeDtypeStruct(a.shap...]
where the time goes in v3:
time: 53.8 us; the launch traced here: 53.6 us
  Pallas kernels  52.8 us (98%)
  between operations  0.8 us (1%)
    pallas_call x1, Pallas kernels, fast_call(): pl.pallas_call(functools.partial(fast_kernel, (S, X, capp)), out_shape=(j...  52 us

profile of v3, /device:TPU:0, one launch (start us, length us, event | category | flops | bytes accessed | tf_op | source)
XLA Modules:
  0.0 53.6 jit_solution(2250047741486607861)
XLA Ops:
  0.6 52.0 %shard_map.140 = (bf16[288,256]{1,0:T(8,128)(2,1)S(1)}, bf16[128,1152]{1,0:T(8,128)(2,1)S(1)}) custom-call(bf16[288,256]{1,0:T(8,128)(2,1)} %bitcast.8, bf16[288,256]{1,0:T(8,128)(2,1)} %bitcast.9, bf16[288,256]{1,0:T(8,128)(2,1)} %bitcast.10, bf16[288,256]{1,0:T(8,128)(2,1)} %bitcast.11, bf16[288,256]{1,0:T(8,128)(2,1)} %bitcast.12, s32[2]{0:T(128)} %flags_hbm.1, ...), custom_call_target="tpu_custom_call" | custom-call | tf_op jit(solution)/shard_map/pallas_call | solution.py:713
  52.7 0.8 %shard_map.141 = (bf16[288,256]{1,0:T(8,128)(2,1)}, bf16[128,1152]{1,0:T(8,128)(2,1)}) custom-call(bf16[288,256]{1,0:T(8,128)(2,1)S(1)} %get-tuple-element.6.attn_ref, bf16[128,1152]{1,0:T(8,128)(2,1)S(1)} %get-tuple-element.7.moe_ref), custom_call_target="tpu_custom_call" | custom-call | tf_op jit(solution)/shard_map/pallas_call | solution.py:693

commit v4 on v3

--- a/solution.py
+++ b/solution.py
@@ -513,9 +513,10 @@
         z_return(src, s).start()
 
     o0, o1, o2, o3 = order
+    landing = [s, mate, jnp.where(inner, far, facing), jnp.where(inner, facing, far)]
     mine(o0)
     turn[...] = jnp.zeros_like(turn)
-    for i, e in enumerate(order):
+    for i, e in enumerate(landing):
         hit = [ids_v[j : j + 1, :] == e for j in range(2)]
         spot = jnp.sum(jnp.where(expert == e, place, 0.0), axis=0, keepdims=True)
         turn[i : i + 1, :] = jnp.where(hit[0] | hit[1], spot, -1.0)
@@ -611,6 +612,10 @@
     def _():
         finish_send(o3)
 
+    @pl.when(inner & (c == 1))
+    def _():
+        finish_send(o2)
+
     @pl.when(inner)
     def _():
         kv_copy(far, 0, facing).wait_recv()
@@ -624,7 +629,7 @@
 
     finish_send(r3)
 
-    @pl.when(inner)
+    @pl.when(inner & (c == 0))
     def _():
         finish_send(o2)
 
@@ -634,16 +639,16 @@
 
     moe[...] = combine(0, finish(s))
     for i in range(1, S - 1):
-        z_return(s, order[i]).wait_recv()
-        moe[...] += combine(i, ret[order[i]])
+        z_return(s, landing[i]).wait_recv()
+        moe[...] += combine(i, ret[landing[i]])
 
     @pl.when(jnp.logical_not(inner))
     def _():
         o_copy().wait_recv()
         attn_ref[...] = o_in[...]
 
-    z_return(s, order[S - 1]).wait_recv()
-    moe_ref[...] = (moe[...] + combine(S - 1, ret[order[S - 1]])).astype(BF16)
+    z_return(s, landing[S - 1]).wait_recv()
+    moe_ref[...] = (moe[...] + combine(S - 1, ret[landing[S - 1]])).astype(BF16)
 
     def drain(i, unused):
         to = lax.rem(s + i, S)

time: 53.8 us -> 53.8 us (level)
  no operation moved by 1% of the time
where the time goes in v4:
time: 53.8 us; the launch traced here: 53.6 us
  Pallas kernels  52.8 us (98%)
  between operations  0.8 us (1%)
    pallas_call x1, Pallas kernels, fast_call(): pl.pallas_call(functools.partial(fast_kernel, (S, X, capp)), out_shape=(j...  52 us

profile of v4, /device:TPU:0, one launch (start us, length us, event | category | flops | bytes accessed | tf_op | source)
XLA Modules:
  0.0 53.6 jit_solution(8621351192045204264)
XLA Ops:
  0.6 52.0 %shard_map.140 = (bf16[288,256]{1,0:T(8,128)(2,1)S(1)}, bf16[128,1152]{1,0:T(8,128)(2,1)S(1)}) custom-call(bf16[288,256]{1,0:T(8,128)(2,1)} %bitcast.8, bf16[288,256]{1,0:T(8,128)(2,1)} %bitcast.9, bf16[288,256]{1,0:T(8,128)(2,1)} %bitcast.10, bf16[288,256]{1,0:T(8,128)(2,1)} %bitcast.11, bf16[288,256]{1,0:T(8,128)(2,1)} %bitcast.12, s32[2]{0:T(128)} %flags_hbm.1, ...), custom_call_target="tpu_custom_call" | custom-call | tf_op jit(solution)/shard_map/pallas_call | solution.py:718
  52.7 0.8 %shard_map.141 = (bf16[288,256]{1,0:T(8,128)(2,1)}, bf16[128,1152]{1,0:T(8,128)(2,1)}) custom-call(bf16[288,256]{1,0:T(8,128)(2,1)S(1)} %get-tuple-element.6.attn_ref, bf16[128,1152]{1,0:T(8,128)(2,1)S(1)} %get-tuple-element.7.moe_ref), custom_call_target="tpu_custom_call" | custom-call | tf_op jit(solution)/shard_map/pallas_call | solution.py:698

commit v5 on v4

--- a/solution.py
+++ b/solution.py
@@ -612,10 +612,6 @@
     def _():
         finish_send(o3)
 
-    @pl.when(inner & (c == 1))
-    def _():
-        finish_send(o2)
-
     @pl.when(inner)
     def _():
         kv_copy(far, 0, facing).wait_recv()
@@ -638,6 +634,11 @@
         return jnp.dot(pick, values, preferred_element_type=F32) * turned[:, S + i : S + i + 1]
 
     moe[...] = combine(0, finish(s))
+
+    @pl.when(inner & (c == 1))
+    def _():
+        finish_send(o2)
+
     for i in range(1, S - 1):
         z_return(s, landing[i]).wait_recv()
         moe[...] += combine(i, ret[landing[i]])

time: 53.8 us -> 53.5 us (level)
  the two profiles are of different devices: /device:TPU:0 before, /device:TPU:13 now
where the time goes in v5:
time: 53.5 us; the launch traced here: 53.4 us
  Pallas kernels  52.6 us (98%)
  between operations  0.8 us (1%)
    pallas_call x1, Pallas kernels, fast_call(): pl.pallas_call(functools.partial(fast_kernel, (S, X, capp)), out_shape=(j...  51.8 us

profile of v5, /device:TPU:13, one launch (start us, length us, event | category | flops | bytes accessed | tf_op | source)
XLA Modules:
  0.0 53.4 jit_solution(4089731377508798035)
XLA Ops:
  0.6 51.8 %shard_map.140 = (bf16[288,256]{1,0:T(8,128)(2,1)S(1)}, bf16[128,1152]{1,0:T(8,128)(2,1)S(1)}) custom-call(bf16[288,256]{1,0:T(8,128)(2,1)} %bitcast.8, bf16[288,256]{1,0:T(8,128)(2,1)} %bitcast.9, bf16[288,256]{1,0:T(8,128)(2,1)} %bitcast.10, bf16[288,256]{1,0:T(8,128)(2,1)} %bitcast.11, bf16[288,256]{1,0:T(8,128)(2,1)} %bitcast.12, s32[2]{0:T(128)} %flags_hbm.1, ...), custom_call_target="tpu_custom_call" | custom-call | tf_op jit(solution)/shard_map/pallas_call | solution.py:719
  52.4 0.8 %shard_map.141 = (bf16[288,256]{1,0:T(8,128)(2,1)}, bf16[128,1152]{1,0:T(8,128)(2,1)}) custom-call(bf16[288,256]{1,0:T(8,128)(2,1)S(1)} %get-tuple-element.6.attn_ref, bf16[128,1152]{1,0:T(8,128)(2,1)S(1)} %get-tuple-element.7.moe_ref), custom_call_target="tpu_custom_call" | custom-call | tf_op jit(solution)/shard_map/pallas_call | solution.py:699
